TPU v7x, 32 devices: a whole 2x2x4 slice. The times are simulated.
32 devices in a mesh: section: 2 (over core), fsdp: 4 (over z), replica: 4 (over y, x).
Axes of the slice: x: 2, y: 2, z: 4, core: 2. Of those that a mesh axis runs over, the one named last changes fastest.
Arguments:
- tokens_in: bfloat16 [2048, 2048], P(('fsdp', 'replica')), may hold values from -6 to 6
- cotangent: bfloat16 [2048, 2048], P(('fsdp', 'replica')), may hold values from -6 to 6
- ln1: bfloat16 [2, 2048], P('section', 'fsdp'), may hold values from 0.25 to 1.75
- wq: bfloat16 [2, 2048, 2048], P('section', 'fsdp'), may hold values from -0.125 to 0.125
- wk: bfloat16 [2, 2048, 1024], P('section', 'fsdp'), may hold values from -0.125 to 0.125
- wv: bfloat16 [2, 2048, 1024], P('section', 'fsdp'), may hold values from -0.125 to 0.125
- qn: bfloat16 [2, 128], P('section', 'fsdp'), may hold values from 0.5 to 2
- kn: bfloat16 [2, 128], P('section', 'fsdp'), may hold values from 0.5 to 2
- wo: bfloat16 [2, 2048, 2048], P('section', 'fsdp'), may hold values from -0.375 to 0.375
- ln2: bfloat16 [2, 2048], P('section', 'fsdp'), may hold values from 0.25 to 1.75
- wg: bfloat16 [2, 2048, 6144], P('section', 'fsdp'), may hold values from -0.125 to 0.125
- wu: bfloat16 [2, 2048, 6144], P('section', 'fsdp'), may hold values from -0.125 to 0.125
- wd: bfloat16 [2, 6144, 2048], P('section', 'fsdp'), may hold values from -0.078125 to 0.078125
Outputs:
- hidden_out: bfloat16 [2, 2048, 2048], P('section', ('fsdp', 'replica'))
- input_grad: float32 [2, 2048, 2048], P('section', ('fsdp', 'replica'))
- grad_ln1: float32 [2, 2048], P('section', 'fsdp')
- grad_wq: float32 [2, 2048, 2048], P('section', 'fsdp')
- grad_wk: float32 [2, 2048, 1024], P('section', 'fsdp')
- grad_wv: float32 [2, 2048, 1024], P('section', 'fsdp')
- grad_qn: float32 [2, 128], P('section', 'fsdp')
- grad_kn: float32 [2, 128], P('section', 'fsdp')
- grad_wo: float32 [2, 2048, 2048], P('section', 'fsdp')
- grad_ln2: float32 [2, 2048], P('section', 'fsdp')
- grad_wg: float32 [2, 2048, 6144], P('section', 'fsdp')
- up_weight_gradient: float32 [2, 2048, 6144], P('section', 'fsdp')
- grad_wd: float32 [2, 6144, 2048], P('section', 'fsdp')
All inputs are finite; a program needn't handle non-finite values.
Results may differ from a plain program's by a relative error of at most 0.028.
Values may be sent and summed in bfloat16 or wider, within the bound.
A program may use at most 448 MiB of HBM per device.

v0:
```python
import math
import jax
import jax.numpy as jnp
from jax import lax
from jax.sharding import PartitionSpec as P

LEN = 128
EPS = 1e-06


def passed_along(value, axis, steps):
    count = lax.axis_size(axis)
    leading, last = (max(0, -steps), min(count, count - steps))
    return lax.ppermute(value, axis, [(source, source + steps) for source in range(leading, last)])


def rope_tables(length, half_dim):
    freq = jnp.exp(jnp.arange(half_dim, dtype=jnp.float32) * (-math.log(1000000.0) / half_dim))
    angle = jnp.arange(length, dtype=jnp.float32)[:, None] * freq[None, :]
    return (jnp.cos(angle), jnp.sin(angle))


def rotate(field, cosine, sine, sign):
    half_dim = field.shape[-1] // 2
    first = field[..., :half_dim]
    second = field[..., half_dim:]
    cosine = cosine[None, :, None, :]
    sine = sign * sine[None, :, None, :]
    return jnp.concatenate(
        [first * cosine - second * sine, second * cosine + first * sine], axis=-1
    )


def head_norm(field, gain):
    factor = lax.rsqrt(jnp.mean(field * field, axis=-1, keepdims=True) + EPS)
    return (field * factor * gain, factor)


def norm_back(field, factor, gain, grad, axes):
    scaled = grad * gain
    back = factor * scaled - field * factor * factor * factor * jnp.mean(
        scaled * field, axis=-1, keepdims=True
    )
    return (back, jnp.sum(grad * field * factor, axis=axes))


def outer(left, right):
    return lax.dot_general(
        left, right, (((0,), (0,)), ((), ())), preferred_element_type=jnp.float32
    )


def against(left, right):
    return lax.dot_general(
        left, right, (((1,), (1,)), ((), ())), preferred_element_type=jnp.float32
    )


def scores_of(qrot, krot):
    length = qrot.shape[1]
    raw = jnp.einsum("sqkgd,smkd->skgqm", qrot, krot, preferred_element_type=jnp.float32)
    raw = raw * (1.0 / math.sqrt(qrot.shape[-1]))
    causal = jnp.arange(length)[:, None] >= jnp.arange(length)[None, :]
    return jnp.where(causal, raw, -jnp.inf)


def forward_parts(x, weights, length):
    ln1, wq, wk, wv, qn, kn, wo, ln2, wg, wu, wd = weights
    rows = x.shape[0]
    seqs = rows // length
    head_dim = qn.shape[0]
    heads = wq.shape[1] // head_dim
    kv_heads = wk.shape[1] // head_dim
    group = heads // kv_heads
    cosine, sine = rope_tables(length, head_dim // 2)
    x32 = x.astype(jnp.float32)
    r1 = lax.rsqrt(jnp.mean(x32 * x32, axis=-1, keepdims=True) + EPS)
    xn = (x32 * r1 * ln1.astype(jnp.float32)).astype(jnp.bfloat16)
    query = jnp.dot(xn, wq, preferred_element_type=jnp.float32).reshape(
        seqs, length, heads, head_dim
    )
    keys = jnp.dot(xn, wk, preferred_element_type=jnp.float32).reshape(
        seqs, length, kv_heads, head_dim
    )
    values = jnp.dot(xn, wv, preferred_element_type=jnp.float32).astype(jnp.bfloat16)
    q_normed, q_factor = head_norm(query, qn.astype(jnp.float32))
    k_normed, k_factor = head_norm(keys, kn.astype(jnp.float32))
    qrot = (
        rotate(q_normed, cosine, sine, 1.0)
        .astype(jnp.bfloat16)
        .reshape(seqs, length, kv_heads, group, head_dim)
    )
    krot = rotate(k_normed, cosine, sine, 1.0).astype(jnp.bfloat16)
    vals = values.reshape(seqs, length, kv_heads, head_dim)
    scores = scores_of(qrot, krot)
    top = jnp.max(scores, axis=-1, keepdims=True)
    lse = top + jnp.log(jnp.sum(jnp.exp(scores - top), axis=-1, keepdims=True))
    weights_p = jnp.exp(scores - lse).astype(jnp.bfloat16)
    attended = jnp.einsum("skgqm,smkd->sqkgd", weights_p, vals, preferred_element_type=jnp.float32)
    attended = attended.astype(jnp.bfloat16).reshape(rows, heads * head_dim)
    hres = x32 + jnp.dot(attended, wo, preferred_element_type=jnp.float32)
    r2 = lax.rsqrt(jnp.mean(hres * hres, axis=-1, keepdims=True) + EPS)
    hn = (hres * r2 * ln2.astype(jnp.float32)).astype(jnp.bfloat16)
    gate = jnp.dot(hn, wg, preferred_element_type=jnp.float32)
    upper = jnp.dot(hn, wu, preferred_element_type=jnp.float32)
    active = (jax.nn.silu(gate) * upper).astype(jnp.bfloat16)
    output = (hres + jnp.dot(active, wd, preferred_element_type=jnp.float32)).astype(jnp.bfloat16)
    return (
        x32,
        r1,
        xn,
        query,
        q_factor,
        keys,
        k_factor,
        vals,
        qrot,
        krot,
        lse,
        attended,
        hres,
        r2,
        hn,
        gate,
        upper,
        active,
        output,
    )


def blank_parts(x, weights, length):
    ln1, wq, wk, wv, qn, kn, wo, ln2, wg, wu, wd = weights
    rows, width = x.shape
    seqs = rows // length
    head_dim = qn.shape[0]
    heads = wq.shape[1] // head_dim
    kv_heads = wk.shape[1] // head_dim
    group = heads // kv_heads
    hidden = wg.shape[1]
    single = jnp.float32
    narrow = jnp.bfloat16
    return (
        jnp.zeros((rows, width), single),
        jnp.zeros((rows, 1), single),
        jnp.zeros((rows, width), narrow),
        jnp.zeros((seqs, length, heads, head_dim), single),
        jnp.zeros((seqs, length, heads, 1), single),
        jnp.zeros((seqs, length, kv_heads, head_dim), single),
        jnp.zeros((seqs, length, kv_heads, 1), single),
        jnp.zeros((seqs, length, kv_heads, head_dim), narrow),
        jnp.zeros((seqs, length, kv_heads, group, head_dim), narrow),
        jnp.zeros((seqs, length, kv_heads, head_dim), narrow),
        jnp.zeros((seqs, kv_heads, group, length, 1), single),
        jnp.zeros((rows, heads * head_dim), narrow),
        jnp.zeros((rows, width), single),
        jnp.zeros((rows, 1), single),
        jnp.zeros((rows, width), narrow),
        jnp.zeros((rows, hidden), single),
        jnp.zeros((rows, hidden), single),
        jnp.zeros((rows, hidden), narrow),
        jnp.zeros((rows, width), narrow),
    )


def act_backward(parts, grad_out, weights, length):
    ln1, wq, wk, wv, qn, kn, wo, ln2, wg, wu, wd = weights
    (
        x32,
        r1,
        xn,
        query,
        q_factor,
        keys,
        k_factor,
        vals,
        qrot,
        krot,
        lse,
        attended,
        hres,
        r2,
        hn,
        gate,
        upper,
        active,
        output,
    ) = parts
    rows = x32.shape[0]
    seqs = rows // length
    head_dim = qn.shape[0]
    heads = wq.shape[1] // head_dim
    kv_heads = wk.shape[1] // head_dim
    group = heads // kv_heads
    cosine, sine = rope_tables(length, head_dim // 2)
    dact = against(grad_out, wd)
    sig = jax.nn.sigmoid(gate)
    d_up = (dact * gate * sig).astype(jnp.bfloat16)
    d_gate = (dact * upper * sig * (1.0 + gate * (1.0 - sig))).astype(jnp.bfloat16)
    d_hn = against(d_gate, wg) + against(d_up, wu)
    dh_norm, d_ln2 = norm_back(hres, r2, ln2.astype(jnp.float32), d_hn, 0)
    d_h = grad_out.astype(jnp.float32) + dh_norm
    d_ab = d_h.astype(jnp.bfloat16)
    d_out = against(d_ab, wo).astype(jnp.bfloat16).reshape(seqs, length, kv_heads, group, head_dim)
    scores = scores_of(qrot, krot)
    probs = jnp.exp(scores - lse)
    probs_b = probs.astype(jnp.bfloat16)
    d_v = jnp.einsum("skgqm,sqkgd->smkd", probs_b, d_out, preferred_element_type=jnp.float32)
    d_vb = d_v.astype(jnp.bfloat16).reshape(rows, kv_heads * head_dim)
    d_p = jnp.einsum("sqkgd,smkd->skgqm", d_out, vals, preferred_element_type=jnp.float32)
    delta = jnp.sum(probs * d_p, axis=-1, keepdims=True)
    d_s = (probs * (d_p - delta) * (1.0 / math.sqrt(head_dim))).astype(jnp.bfloat16)
    d_qrot = jnp.einsum("skgqm,smkd->sqkgd", d_s, krot, preferred_element_type=jnp.float32).reshape(
        seqs, length, heads, head_dim
    )
    d_krot = jnp.einsum("skgqm,sqkgd->smkd", d_s, qrot, preferred_element_type=jnp.float32)
    d_qh = rotate(d_qrot, cosine, sine, -1.0)
    d_kh = rotate(d_krot, cosine, sine, -1.0)
    d_q, d_qn = norm_back(query, q_factor, qn.astype(jnp.float32), d_qh, (0, 1, 2))
    d_k, d_kn = norm_back(keys, k_factor, kn.astype(jnp.float32), d_kh, (0, 1, 2))
    d_qb = d_q.astype(jnp.bfloat16).reshape(rows, heads * head_dim)
    d_kb = d_k.astype(jnp.bfloat16).reshape(rows, kv_heads * head_dim)
    d_xn = against(d_qb, wq) + against(d_kb, wk) + against(d_vb, wv)
    dx_norm, d_ln1 = norm_back(x32, r1, ln1.astype(jnp.float32), d_xn, 0)
    d_x = d_h + dx_norm
    saved = (xn, d_qb, d_kb, d_vb, attended, d_ab, hn, d_gate, d_up, active, grad_out)
    return (d_x, saved, (d_ln1, d_qn, d_kn, d_ln2))


def blank_backward(x, weights):
    ln1, wq, wk, wv, qn, kn, wo, ln2, wg, wu, wd = weights
    rows, width = x.shape

    def empty(columns):
        return jnp.zeros((rows, columns), jnp.bfloat16)

    saved = (
        empty(width),
        empty(wq.shape[1]),
        empty(wk.shape[1]),
        empty(wv.shape[1]),
        empty(wq.shape[1]),
        empty(width),
        empty(width),
        empty(wg.shape[1]),
        empty(wg.shape[1]),
        empty(wg.shape[1]),
        empty(width),
    )
    small = (
        jnp.zeros((width,), jnp.float32),
        jnp.zeros((qn.shape[0],), jnp.float32),
        jnp.zeros((qn.shape[0],), jnp.float32),
        jnp.zeros((width,), jnp.float32),
    )
    return (jnp.zeros((rows, width), jnp.float32), saved, small)


def per_device(tokens_in, cotangent, ln1, wq, wk, wv, qn, kn, wo, ln2, wg, wu, wd):
    relay_section = lax.axis_index("section")
    shards = (ln1[0], wq[0], wk[0], wv[0], qn[0], kn[0], wo[0], ln2[0], wg[0], wu[0], wd[0])
    gathered = (
        lax.all_gather(shards[0], "fsdp", axis=0, tiled=True),
        lax.all_gather(shards[1], "fsdp", axis=0, tiled=True),
        lax.all_gather(shards[2], "fsdp", axis=0, tiled=True),
        lax.all_gather(shards[3], "fsdp", axis=0, tiled=True),
        lax.all_gather(shards[4], "fsdp", axis=0, tiled=True),
        lax.all_gather(shards[5], "fsdp", axis=0, tiled=True),
        lax.all_gather(shards[6], "fsdp", axis=0, tiled=True),
        lax.all_gather(shards[7], "fsdp", axis=0, tiled=True),
        lax.all_gather(shards[8], "fsdp", axis=0, tiled=True),
        lax.all_gather(shards[9], "fsdp", axis=0, tiled=True),
        lax.all_gather(shards[10], "fsdp", axis=0, tiled=True),
    )

    def forward_execute(layer_in):
        return forward_parts(layer_in, gathered, LEN)

    def skip_forward(layer_in):
        return blank_parts(layer_in, gathered, LEN)

    first_parts = lax.cond(relay_section == 0, forward_execute, skip_forward, tokens_in)
    first = first_parts[-1]
    passed = passed_along(first, "section", 1)
    second_parts = lax.cond(relay_section == 1, forward_execute, skip_forward, passed)
    hidden_out = jnp.where(relay_section == 0, first, second_parts[-1])

    def run_backward(pair):
        return act_backward(pair[0], pair[1], gathered, LEN)

    def skip_backward(pair):
        return blank_backward(pair[0][0], gathered)

    late = lax.cond(relay_section == 1, run_backward, skip_backward, (second_parts, cotangent))
    sent = passed_along(late[0].astype(jnp.bfloat16), "section", -1)
    early = lax.cond(relay_section == 0, run_backward, skip_backward, (first_parts, sent))
    picked = jax.tree.map(
        lambda left, right: jnp.where(relay_section == 0, left, right), early, late
    )
    input_grad = picked[0]
    xn, d_qb, d_kb, d_vb, attended, d_ab, hn, d_gate, d_up, active, grad_out = picked[1]
    d_ln1, d_qn, d_kn, d_ln2 = picked[2]
    lefts = (
        lax.all_to_all(xn, "fsdp", split_axis=1, concat_axis=0, tiled=True),
        lax.all_to_all(attended, "fsdp", split_axis=1, concat_axis=0, tiled=True),
        lax.all_to_all(hn, "fsdp", split_axis=1, concat_axis=0, tiled=True),
        lax.all_to_all(active, "fsdp", split_axis=1, concat_axis=0, tiled=True),
    )
    rights = (
        lax.all_gather(d_qb, "fsdp", axis=0, tiled=True),
        lax.all_gather(d_kb, "fsdp", axis=0, tiled=True),
        lax.all_gather(d_vb, "fsdp", axis=0, tiled=True),
        lax.all_gather(d_ab, "fsdp", axis=0, tiled=True),
        lax.all_gather(d_gate, "fsdp", axis=0, tiled=True),
        lax.all_gather(d_up, "fsdp", axis=0, tiled=True),
        lax.all_gather(grad_out, "fsdp", axis=0, tiled=True),
    )
    gains = (
        lax.psum_scatter(d_ln1, "fsdp", scatter_dimension=0, tiled=True),
        lax.psum_scatter(d_qn, "fsdp", scatter_dimension=0, tiled=True),
        lax.psum_scatter(d_kn, "fsdp", scatter_dimension=0, tiled=True),
        lax.psum_scatter(d_ln2, "fsdp", scatter_dimension=0, tiled=True),
    )
    local = (
        gains[0],
        outer(lefts[0], rights[0]),
        outer(lefts[0], rights[1]),
        outer(lefts[0], rights[2]),
        gains[1],
        gains[2],
        outer(lefts[1], rights[3]),
        gains[3],
        outer(lefts[2], rights[4]),
        outer(lefts[2], rights[5]),
        outer(lefts[3], rights[6]),
    )
    owned = (
        lax.psum(local[0].astype(jnp.bfloat16), "replica").astype(jnp.float32),
        lax.psum(local[1].astype(jnp.bfloat16), "replica").astype(jnp.float32),
        lax.psum(local[2].astype(jnp.bfloat16), "replica").astype(jnp.float32),
        lax.psum(local[3].astype(jnp.bfloat16), "replica").astype(jnp.float32),
        lax.psum(local[4].astype(jnp.bfloat16), "replica").astype(jnp.float32),
        lax.psum(local[5].astype(jnp.bfloat16), "replica").astype(jnp.float32),
        lax.psum(local[6].astype(jnp.bfloat16), "replica").astype(jnp.float32),
        lax.psum(local[7].astype(jnp.bfloat16), "replica").astype(jnp.float32),
        lax.psum(local[8].astype(jnp.bfloat16), "replica").astype(jnp.float32),
        lax.psum(local[9].astype(jnp.bfloat16), "replica").astype(jnp.float32),
        lax.psum(local[10].astype(jnp.bfloat16), "replica").astype(jnp.float32),
    )
    return (
        hidden_out[None],
        input_grad[None],
        owned[0][None],
        owned[1][None],
        owned[2][None],
        owned[3][None],
        owned[4][None],
        owned[5][None],
        owned[6][None],
        owned[7][None],
        owned[8][None],
        owned[9][None],
        owned[10][None],
    )


def solution(mesh):
    return jax.shard_map(
        per_device,
        mesh=mesh,
        in_specs=(
            P(("fsdp", "replica"), None),
            P(("fsdp", "replica"), None),
            P("section", "fsdp"),
            P("section", "fsdp", None),
            P("section", "fsdp", None),
            P("section", "fsdp", None),
            P("section", "fsdp"),
            P("section", "fsdp"),
            P("section", "fsdp", None),
            P("section", "fsdp"),
            P("section", "fsdp", None),
            P("section", "fsdp", None),
            P("section", "fsdp", None),
        ),
        out_specs=(
            P("section", ("fsdp", "replica"), None),
            P("section", ("fsdp", "replica"), None),
            P("section", "fsdp"),
            P("section", "fsdp", None),
            P("section", "fsdp", None),
            P("section", "fsdp", None),
            P("section", "fsdp"),
            P("section", "fsdp"),
            P("section", "fsdp", None),
            P("section", "fsdp"),
            P("section", "fsdp", None),
            P("section", "fsdp", None),
            P("section", "fsdp", None),
        ),
        check_vma=False,
    )
```

profile of v0, /device:TPU:0, one launch (start us, length us, event | category | flops | bytes accessed | tf_op | source)
XLA Modules:
  0.0 3080.5 jit_solution(9624293792412232464)
XLA Ops:
  12.0 13.8 all-gather
  25.8 13.2 all-gather.7
  40.8 9.8 all-reduce.9
  50.7 42.8 %all-gather.42.cloned.1.call-done = bf16[1,2048,1024]{2,1,0:T(8,128)(2,1)} async-done(((bf16[1,512,1024]{2,1,0:T(8,128)(2,1)}), bf16[1,2048,1024]{2,1,0:T(8,128)(2,1)}) %all-gather.42.cloned.1.call-update) | async-done | bytes 4194320 | tf_op jit(solution)/shard_map/all_gather | solution.py:264
  93.4 80.9 %all-gather.44.cloned.1.call-done = bf16[1,2048,1024]{2,1,0:T(8,128)(2,1)} async-done(((bf16[1,512,1024]{2,1,0:T(8,128)(2,1)}), bf16[1,2048,1024]{2,1,0:T(8,128)(2,1)}) %all-gather.44.cloned.1.call-update) | async-done | bytes 4194320 | tf_op jit(solution)/shard_map/all_gather | solution.py:265
  174.3 149.7 %all-gather.40.cloned.1.call-done = bf16[1,2048,2048]{2,1,0:T(8,128)(2,1)} async-done(((bf16[1,512,2048]{2,1,0:T(8,128)(2,1)}), bf16[1,2048,2048]{2,1,0:T(8,128)(2,1)}) %all-gather.40.cloned.1.call-update) | async-done | bytes 8388624 | tf_op jit(solution)/shard_map/all_gather | solution.py:263
  324.0 149.3 %all-gather.46.cloned.1.call-done = bf16[1,2048,2048]{2,1,0:T(8,128)(2,1)} async-done(((bf16[1,512,2048]{2,1,0:T(8,128)(2,1)}), bf16[1,2048,2048]{2,1,0:T(8,128)(2,1)}) %all-gather.46.cloned.1.call-update) | async-done | bytes 8388624 | tf_op jit(solution)/shard_map/all_gather | solution.py:268
  473.3 424.8 %all-gather.48.cloned.1.call-done = bf16[1,2048,6144]{2,1,0:T(8,128)(2,1)} async-done(((bf16[1,512,6144]{2,1,0:T(8,128)(2,1)}), bf16[1,2048,6144]{2,1,0:T(8,128)(2,1)}) %all-gather.48.cloned.1.call-update) | async-done | bytes 25165840 | tf_op jit(solution)/shard_map/all_gather | solution.py:270
  898.1 424.8 %all-gather.50.cloned.1.call-done = bf16[1,2048,6144]{2,1,0:T(8,128)(2,1)} async-done(((bf16[1,512,6144]{2,1,0:T(8,128)(2,1)}), bf16[1,2048,6144]{2,1,0:T(8,128)(2,1)}) %all-gather.50.cloned.1.call-update) | async-done | bytes 25165840 | tf_op jit(solution)/shard_map/all_gather | solution.py:271
  1322.9 425.0 %all-gather.52.cloned.1.call-done = bf16[1,6144,2048]{2,1,0:T(8,128)(2,1)} async-done(((bf16[1,1536,2048]{2,1,0:T(8,128)(2,1)}), bf16[1,6144,2048]{2,1,0:T(8,128)(2,1)}) %all-gather.52.cloned.1.call-update) | async-done | bytes 25165840 | tf_op jit(solution)/shard_map/all_gather | solution.py:272
  1747.8 67.8 %conditional.4 = (f32[128,2048]{1,0:T(8,128)S(1)}, f32[128,1]{0,1:T(1,128)S(1)}, bf16[128,2048]{1,0:T(8,128)(2,1)}, f32[1,128,16,128]{3,2,1,0:T(8,128)S(1)}, f32...) conditional(s32[]{:T(128)} %convert_element_type.277, () %tuple.40, ...), branch_computations={%region_0.0_spmd, %region_1.8_spmd} | conditional | flops 13036057600 | bytes 192852512 | solution.py:281
  1748.7 5.0 convolution_bitcast_fusion
  1764.9 5.8 multiply_reduce_fusion
  1772.1 13.6 fusion.84
  1785.8 15.1 multiply_convert_fusion
  1800.9 13.2 fusion
  1818.8 25.6 conditional.5
  1844.9 23.1 conditional.6
  1869.4 161.2 %collective-permute-done.1 = bf16[128,2048]{1,0:T(8,128)(2,1)} collective-permute-done((bf16[128,2048]{1,0:T(8,128)(2,1)S(1)}, bf16[128,2048]{1,0:T(8,128)(2,1)}, u32[]{:S(2)}, u32[]{:S(2)}) %collective-permute-start.1) | collective-permute-done | bytes 524320 | tf_op jit(solution)/shard_map/ppermute | solution.py:14
  2030.6 108.4 %conditional.7 = (bf16[128,2048]{0,1:T(8,128)(2,1)}, bf16[128,1024]{0,1:T(8,128)(2,1)}, bf16[128,1024]{0,1:T(8,128)(2,1)}, f32[2048]{0:T(1024)S(1)}, f32[128]{0:...) conditional(s32[]{:T(128)} %convert_element_type.277, () %tuple.44, ...), branch_computations={%region_27.28_spmd, %region_28.38_spmd} | conditional | flops 13252196352 | bytes 250843936 | solution.py:295
  2032.0 15.8 multiply_convert_fusion.9
  2047.8 14.1 fusion.88
  2061.9 15.0 multiply_reduce_fusion.17
  2079.8 7.1 convolution_convert_fusion.5
  2108.2 6.6 fusion.89
  2160.4 13.3 all-to-all-done
  2173.7 3.5 all-to-all-start.1
  2179.1 17.4 all-to-all-done.1
  2196.5 3.5 all-to-all-start.2
  2202.7 9.4 all-to-all-done.2
  2212.2 3.6 all-to-all-start.3
  2225.0 43.9 %all-to-all-done.3 = bf16[128,4,1536]{0,2,1:T(8,128)(2,1)S(1)} async-done(((bf16[128,4,1536]{0,2,1:T(8,128)(2,1)}), bf16[128,4,1536]{0,2,1:T(8,128)(2,1)S(1)}, u32[]{:S(2)}, u32[]{:S(2)}) %all-to-all-start.3) | async-done | bytes 1572896 | tf_op jit(solution)/shard_map/all_to_all | solution.py:306
  2271.2 4.4 fusion.75
  2275.6 42.4 %all-gather.32.cloned.1.call-done = bf16[512,2048]{0,1:T(8,128)(2,1)} async-done(((bf16[128,2048]{0,1:T(8,128)(2,1)}), bf16[512,2048]{0,1:T(8,128)(2,1)}) %all-gather.32.cloned.1.call-update) | async-done | bytes 2097168 | tf_op jit(solution)/shard_map/all_gather | solution.py:312
  2318.0 4.2 fusion.76
  2322.2 41.7 %all-gather.38.cloned.1.call-done = bf16[512,2048]{0,1:T(8,128)(2,1)} async-done(((bf16[128,2048]{0,1:T(8,128)(2,1)}), bf16[512,2048]{0,1:T(8,128)(2,1)}) %all-gather.38.cloned.1.call-update) | async-done | bytes 2097168 | tf_op jit(solution)/shard_map/all_gather | solution.py:315
  2363.9 7.0 fusion.74
  2370.9 108.1 %all-gather.34.cloned.1.call-done = bf16[512,6144]{0,1:T(8,128)(2,1)} async-done(((bf16[128,6144]{0,1:T(8,128)(2,1)}), bf16[512,6144]{0,1:T(8,128)(2,1)}) %all-gather.34.cloned.1.call-update) | async-done | bytes 6291472 | tf_op jit(solution)/shard_map/all_gather | solution.py:313
  2479.1 8.2 fusion.72
  2487.3 106.8 %all-gather.36.cloned.1.call-done = bf16[512,6144]{0,1:T(8,128)(2,1)} async-done(((bf16[128,6144]{0,1:T(8,128)(2,1)}), bf16[512,6144]{0,1:T(8,128)(2,1)}) %all-gather.36.cloned.1.call-update) | async-done | bytes 6291472 | tf_op jit(solution)/shard_map/all_gather | solution.py:314
  2594.1 8.2 fusion.73
  2608.2 16.7 all-reduce.6
  2625.2 10.3 all-reduce.7
  2637.7 406.8 %all-reduce.12.cloned.1.call-done = (bf16[1,512,2048]{2,1,0:T(8,128)(2,1)}, bf16[1,512,1024]{2,1,0:T(8,128)(2,1)}, bf16[1,512,1024]{2,1,0:T(8,128)(2,1)}, bf16[1...) async-done(((bf16[1,512,2048]{2,1,0:T(8,128)(2,1)}, bf16[1,512,1024]{2,1,0:T(8,128)(2,1)}, ...) | async-done | bytes 25165840 | tf_op jit(solution)/shard_map/psum | solution.py:338
  3044.5 4.3 broadcast_in_dim.173
  3054.6 6.4 broadcast_in_dim.187
  3061.0 6.4 broadcast_in_dim.189
  3067.5 6.3 broadcast_in_dim.191
  (334 shorter events, 152.8 us)
Async XLA Ops:
  7.2 86.2 %all-gather.42.cloned.1.call-start = ((), (), s32[]{:S(2)}) async-start(), calls=%async_computation.12 | async-start | bytes 5242880 | tf_op jit(solution)/shard_map/all_gather | solution.py:264
  7.9 166.4 %all-gather.44.cloned.1.call-start = ((), (), s32[]{:S(2)}) async-start(), calls=%async_computation.13 | async-start | bytes 5242880 | tf_op jit(solution)/shard_map/all_gather | solution.py:265
  8.7 315.3 %all-gather.40.cloned.1.call-start = ((), (), s32[]{:S(2)}) async-start(), calls=%async_computation.11 | async-start | bytes 10485760 | tf_op jit(solution)/shard_map/all_gather | solution.py:263
  9.4 463.9 %all-gather.46.cloned.1.call-start = ((), (), s32[]{:S(2)}) async-start(), calls=%async_computation.14 | async-start | bytes 10485760 | tf_op jit(solution)/shard_map/all_gather | solution.py:268
  10.0 888.1 %all-gather.48.cloned.1.call-start = ((), (), s32[]{:S(2)}) async-start(), calls=%async_computation.15 | async-start | bytes 31457280 | tf_op jit(solution)/shard_map/all_gather | solution.py:270
  10.6 1312.3 %all-gather.50.cloned.1.call-start = ((), (), s32[]{:S(2)}) async-start(), calls=%async_computation.16 | async-start | bytes 31457280 | tf_op jit(solution)/shard_map/all_gather | solution.py:271
  11.1 14.7 copy-start.73
  11.2 27.9 copy-start.74
  11.2 29.2 copy-start.85
  11.2 29.4 copy-start.86
  11.2 1736.6 %copy-start.50 = (bf16[128,2048]{1,0:T(8,128)(2,1)S(1)}, bf16[128,2048]{1,0:T(8,128)(2,1)}, u32[]{:S(2)}) copy-start(bf16[128,2048]{1,0:T(8,128)(2,1)} %param.21) | copy-start | bytes 1572868
  11.2 1736.6 %all-gather.52.cloned.1.call-start = ((), (), s32[]{:S(2)}) async-start(), calls=%async_computation.17 | async-start | bytes 31457280 | tf_op jit(solution)/shard_map/all_gather | solution.py:272
  11.9 2206.9 %all-gather.28.cloned.1.call-start = ((), (), s32[]{:S(2)}) async-start(), calls=%async_computation.5 | async-start | bytes 1310720 | tf_op jit(solution)/shard_map/all_gather | solution.py:310
  50.7 1768.1 %copy-start.87 = (bf16[128]{0:T(256)(128)(2,1)}, bf16[128]{0:T(256)(128)(2,1)S(1)}, u32[]{:S(2)}) copy-start(bf16[128]{0:T(256)(128)(2,1)S(1)} %get-tuple-element.1148) | copy-start | bytes 772
  50.7 1768.1 %copy-start.90 = (bf16[128]{0:T(256)(128)(2,1)}, bf16[128]{0:T(256)(128)(2,1)S(1)}, u32[]{:S(2)}) copy-start(bf16[128]{0:T(256)(128)(2,1)S(1)} %get-tuple-element.1149) | copy-start | bytes 772
  1748.5 16.3 copy-start.6
  1748.7 6.8 copy-start.12
  1764.3 6.4 copy-start.57
  1764.8 7.3 copy-start.30
  1772.1 13.6 copy-start.32
  1800.9 14.5 copy-start.7
  1800.9 14.5 copy-start.11
  1815.7 3.0 collective-permute-start
  1844.9 185.7 %copy-start.56 = (f32[1,128,16,1]{2,1,3,0:T(8,128)S(1)}, f32[1,128,16,1]{2,1,3,0:T(8,128)}, u32[]{:S(2)}) copy-start(f32[1,128,16,1]{2,1,3,0:T(8,128)} %copy-done.55) | copy-start | bytes 24580
  1868.0 162.6 %copy-start.19 = (f32[128,2048]{1,0:T(8,128)}, f32[128,2048]{1,0:T(8,128)S(1)}, u32[]{:S(2)}) copy-start(f32[128,2048]{1,0:T(8,128)S(1)} %get-tuple-element.355) | copy-start | bytes 3145732
  1868.1 162.5 %collective-permute-start.1 = (bf16[128,2048]{1,0:T(8,128)(2,1)S(1)}, bf16[128,2048]{1,0:T(8,128)(2,1)}, u32[]{:S(2)}, u32[]{:S(2)}) collective-permute-start(bf16[128,2048]{1,0:T(8,128)(2,1)S(1)} %convert_element_type.279), channel_id=1, source_target_pairs={{16,0},{17,1},{18,2},{19,3},{20,4},{21,5},{22,6},{23,7},{24,8},{25... | collective-permute-start | bytes 1572872 | tf_op jit(solution)/shard_map/ppermute | solution.py:14
  2047.8 14.1 copy-start.68
  2088.2 6.8 copy-start.36
  2108.2 6.6 copy-start.3
  2132.7 6.2 copy-start.84
  2140.7 81.3 %all-gather.30.cloned.1.call-start = ((), (), s32[]{:S(2)}) async-start(), calls=%async_computation.6 | async-start | bytes 1310720 | tf_op jit(solution)/shard_map/all_gather | solution.py:311
  2142.5 128.7 %all-gather.26.cloned.1.call-start = ((), (), s32[]{:S(2)}) async-start(), calls=%async_computation.4 | async-start | bytes 2621440 | tf_op jit(solution)/shard_map/all_gather | solution.py:309
  2144.5 173.5 %all-gather.32.cloned.1.call-start = ((), (), s32[]{:S(2)}) async-start(), calls=%async_computation.7 | async-start | bytes 2621440 | tf_op jit(solution)/shard_map/all_gather | solution.py:312
  2146.5 217.4 %all-gather.38.cloned.1.call-start = ((), (), s32[]{:S(2)}) async-start(), calls=%async_computation.10 | async-start | bytes 2621440 | tf_op jit(solution)/shard_map/all_gather | solution.py:315
  2148.5 330.6 %all-gather.34.cloned.1.call-start = ((), (), s32[]{:S(2)}) async-start(), calls=%async_computation.8 | async-start | bytes 7864320 | tf_op jit(solution)/shard_map/all_gather | solution.py:313
  2151.3 442.8 %all-gather.36.cloned.1.call-start = ((), (), s32[]{:S(2)}) async-start(), calls=%async_computation.9 | async-start | bytes 7864320 | tf_op jit(solution)/shard_map/all_gather | solution.py:314
  2156.0 17.7 all-to-all-start
  2173.7 22.8 all-to-all-start.1
  2196.5 15.7 all-to-all-start.2
  2212.2 56.8 %all-to-all-start.3 = ((bf16[128,4,1536]{0,2,1:T(8,128)(2,1)}), bf16[128,4,1536]{0,2,1:T(8,128)(2,1)S(1)}, u32[]{:S(2)}, u32[]{:S(2)}) async-start(bf16[128,4,1536]{0,2,1:T(8,128)(2,1)} %bitcast.171), calls=%async_computation.3 | async-start | bytes 3145728 | tf_op jit(solution)/shard_map/all_to_all | solution.py:306
  2215.7 828.7 %all-reduce.12.cloned.1.call-start = ((), (), s32[]{:S(2)}) async-start(), calls=%async_computation.18 | async-start | bytes 50331648 | tf_op jit(solution)/shard_map/psum | solution.py:338
  2269.7 48.3 %copy-start.53 = (bf16[4,128,512]{2,1,0:T(8,128)(2,1)S(1)}, bf16[4,128,512]{2,1,0:T(8,128)(2,1)}, u32[]{:S(2)}) copy-start(bf16[4,128,512]{2,1,0:T(8,128)(2,1)} %copy.319) | copy-start | bytes 1572868
  2363.9 115.2 %copy-start.52 = (bf16[4,128,512]{2,1,0:T(8,128)(2,1)S(1)}, bf16[4,128,512]{2,1,0:T(8,128)(2,1)}, u32[]{:S(2)}) copy-start(bf16[4,128,512]{2,1,0:T(8,128)(2,1)} %copy.324) | copy-start | bytes 1572868
  3044.5 10.1 slice-start.4
  3051.9 9.1 slice-start.2
  3054.6 6.4 slice-start.3
  3054.6 12.9 slice-start
  3061.0 6.4 slice-start.1
  (42 other events, 143.7 us)
Sparse Core Ops, SparseCore 0:
  9.6 83.8 all-gather.41
  95.0 79.2 all-gather.43
  175.9 148.0 all-gather.39
  325.4 147.7 all-gather.45
  474.7 423.3 all-gather.47
  899.5 423.3 all-gather.49
  1324.5 423.3 all-gather.51
  2140.9 31.9 all-gather.27
  2174.4 34.9 all-gather.29
  2211.4 59.7 all-gather.25
  2272.7 45.2 all-gather.31
  2319.4 44.4 all-gather.37
  2366.0 112.9 all-gather.33
  2481.1 112.9 all-gather.35
  2602.4 441.9 all-reduce.11
where the time goes:
time: 3090 us; the launch traced here: 3080 us
  waiting for transfers between devices  2660 us (86%)
  matrix products  167 us (5%)
  other arithmetic  75.6 us (2%)
  blocking collectives  63.8 us (2%)
  local copies, waits for them, and re-layouts  62.9 us (2%)
    all_gather x1, waiting for transfers between devices, per_device(): lax.all_gather(shards[10], 'fsdp', axis=0, tiled=True)  425 us
    all_gather x1, waiting for transfers between devices, per_device(): lax.all_gather(shards[9], 'fsdp', axis=0, tiled=True)  425 us
    all_gather x1, waiting for transfers between devices, per_device(): lax.all_gather(shards[8], 'fsdp', axis=0, tiled=True)  425 us
    psum x1, waiting for transfers between devices, per_device(): lax.psum(local[1].astype(jnp.bfloat16), 'replica').astype(jnp.float32)  407 us
    ppermute x2, waiting for transfers between devices, passed_along(): lax.ppermute(value, axis, [(source, source + steps) for source in range(l...  163 us
    all_gather x1, waiting for transfers between devices, per_device(): lax.all_gather(shards[1], 'fsdp', axis=0, tiled=True)  150 us
    all_gather x1, waiting for transfers between devices, per_device(): lax.all_gather(shards[6], 'fsdp', axis=0, tiled=True)  149 us
    all_gather x1, waiting for transfers between devices, per_device(): lax.all_gather(d_gate, 'fsdp', axis=0, tiled=True)  108 us
  transfers between devices with their start and end apart: 21, of which 19 were waited for; matrix products, arithmetic and copies ran while one was open for 2% of the time, Pallas kernels for 0%

commit v1 on v0

--- a/solution.py
+++ b/solution.py
@@ -6,6 +6,19 @@
 
 LEN = 128
 EPS = 1e-06
+
+
+def gather_around(x, axis, dim):
+    ways = lax.axis_size(axis)
+    up = [(d, (d + 1) % ways) for d in range(ways)]
+    down = [(d, (d - 1) % ways) for d in range(ways)]
+    earlier, later = ([x], [x])
+    for _ in range(ways // 2):
+        earlier.append(lax.ppermute(earlier[-1], axis, up))
+    for _ in range((ways - 1) // 2):
+        later.append(lax.ppermute(later[-1], axis, down))
+    line = jnp.concatenate([*earlier[::-1], *later[1:]], axis=dim)
+    return jnp.roll(line, (lax.axis_index(axis) - ways // 2) * x.shape[dim], axis=dim)
 
 
 def passed_along(value, axis, steps):
@@ -269,7 +282,7 @@
         lax.all_gather(shards[7], "fsdp", axis=0, tiled=True),
         lax.all_gather(shards[8], "fsdp", axis=0, tiled=True),
         lax.all_gather(shards[9], "fsdp", axis=0, tiled=True),
-        lax.all_gather(shards[10], "fsdp", axis=0, tiled=True),
+        gather_around(shards[10], "fsdp", 0),
     )
 
     def forward_execute(layer_in):

time: 3090 us -> 3030 us (0.981)
  waiting for transfers between devices: 2660 us -> 1980 us
  blocking collectives: 63.8 us -> 576 us
  local copies, waits for them, and re-layouts: 62.9 us -> 135 us
    all_gather x1, blocking collectives: 13.8 us -> 518 us  [per_device(): lax.all_gather(shards[0], 'fsdp', axis=0, tiled=True)]
    all_gather x1 -> x0, waiting for transfers between devices: 425 us -> none  [per_device(): lax.all_gather(shards[10], 'fsdp', axis=0, tiled=True)]
    ppermute x0 -> x3, waiting for transfers between devices: none -> 253 us  [the longest x2 253 us: gather_around(): earlier.append(lax.ppermute(earlier[-1], axis, up))]
    all_gather x1, waiting for transfers between devices: 150 us -> 0.01 us  [per_device(): lax.all_gather(shards[1], 'fsdp', axis=0, tiled=True)]
    all_gather x1, waiting for transfers between devices: 149 us -> 0.01 us  [per_device(): lax.all_gather(shards[6], 'fsdp', axis=0, tiled=True)]
    all_gather x1, waiting for transfers between devices: 80.9 us -> 0.01 us  [per_device(): lax.all_gather(shards[3], 'fsdp', axis=0, tiled=True)]
    all_gather x1, waiting for transfers between devices: 425 us -> 345 us  [per_device(): lax.all_gather(shards[8], 'fsdp', axis=0, tiled=True)]
    all_gather x1, waiting for transfers between devices: 42.8 us -> 0.01 us  [per_device(): lax.all_gather(shards[2], 'fsdp', axis=0, tiled=True)]
  transfers between devices with their start and end apart: 21 -> 23, of which waited for: 19 -> 15; matrix products, arithmetic and copies ran while one was open for 2% -> 4% of each run, Pallas kernels for 0% -> 0%
where the time goes in v1:
time: 3030 us; the launch traced here: 3020 us
  waiting for transfers between devices  1980 us (65%)
  blocking collectives  576 us (19%)
  matrix products  168 us (6%)
  local copies, waits for them, and re-layouts  135 us (4%)
  other arithmetic  85.7 us (3%)
  starting transfers between devices  42.8 us (1%)
    all_gather x1, blocking collectives, per_device(): lax.all_gather(shards[0], 'fsdp', axis=0, tiled=True)  518 us
    all_gather x1, waiting for transfers between devices, per_device(): lax.all_gather(shards[9], 'fsdp', axis=0, tiled=True)  425 us
    psum x1, waiting for transfers between devices, per_device(): lax.psum(local[1].astype(jnp.bfloat16), 'replica').astype(jnp.float32)  405 us
    all_gather x1, waiting for transfers between devices, per_device(): lax.all_gather(shards[8], 'fsdp', axis=0, tiled=True)  345 us
    ppermute x2, waiting for transfers between devices, gather_around(): earlier.append(lax.ppermute(earlier[-1], axis, up))  253 us
    ppermute x2, waiting for transfers between devices, passed_along(): lax.ppermute(value, axis, [(source, source + steps) for source in range(l...  159 us
    all_gather x1, waiting for transfers between devices, per_device(): lax.all_gather(d_up, 'fsdp', axis=0, tiled=True)  108 us
    all_gather x1, waiting for transfers between devices, per_device(): lax.all_gather(d_gate, 'fsdp', axis=0, tiled=True)  107 us
  transfers between devices with their start and end apart: 23, of which 15 were waited for; matrix products, arithmetic and copies ran while one was open for 4% of the time, Pallas kernels for 0%

profile of v1, /device:TPU:0, one launch (start us, length us, event | category | flops | bytes accessed | tf_op | source)
XLA Modules:
  0.0 3020.7 jit_solution(362967003791450053)
XLA Ops:
  14.3 252.7 %collective-permute-done = bf16[1536,2048]{1,0:T(8,128)(2,1)} collective-permute-done((bf16[1536,2048]{1,0:T(8,128)(2,1)}, bf16[1536,2048]{1,0:T(8,128)(2,1)}, u32[]{:S(2)}, u32[]{:S(2)}) %collective-permute-start) | collective-permute-done | bytes 6291488 | tf_op jit(solution)/shard_map/ppermute | solution.py:17
  267.1 18.7 collective-permute-start.1
  288.8 517.9 %all-gather = bf16[1,2048]{1,0:T(2,128)(2,1)S(1)} all-gather(bf16[1,512]{1,0:T(2,128)(2,1)S(1)} %copy-done.87), channel_id=2, replica_groups=mesh['section'=2,'fsdp'=4,'replica'=4] {'fsdp'}, dimensions={1}, use_global_device_ids=true | all-gather | bytes 5120 | tf_op jit(solution)/shard_map/all_gather | solution.py:275
  806.7 21.1 all-gather.7
  829.6 9.8 all-reduce.9
  839.4 8.3 constant_dynamic-update-slice_fusion.7
  847.7 7.4 constant_dynamic-update-slice_fusion.6
  858.2 6.6 constant_dynamic-update-slice_fusion.4
  864.8 6.5 constant_dynamic-update-slice_fusion.3
  871.4 6.6 constant_dynamic-update-slice_fusion.2
  881.1 6.5 constant_dynamic-update-slice_fusion
  887.7 22.5 constant_dynamic-slice_fusion
  910.2 344.7 %all-gather.46.cloned.1.call-done = bf16[1,2048,6144]{2,1,0:T(8,128)(2,1)} async-done(((bf16[1,512,6144]{2,1,0:T(8,128)(2,1)}), bf16[1,2048,6144]{2,1,0:T(8,128)(2,1)}) %all-gather.46.cloned.1.call-update) | async-done | bytes 25165840 | tf_op jit(solution)/shard_map/all_gather | solution.py:283
  1254.9 424.8 %all-gather.48.cloned.1.call-done = bf16[1,2048,6144]{2,1,0:T(8,128)(2,1)} async-done(((bf16[1,512,6144]{2,1,0:T(8,128)(2,1)}), bf16[1,2048,6144]{2,1,0:T(8,128)(2,1)}) %all-gather.48.cloned.1.call-update) | async-done | bytes 25165840 | tf_op jit(solution)/shard_map/all_gather | solution.py:284
  1679.7 71.1 %conditional.4 = (f32[128,2048]{1,0:T(8,128)S(1)}, f32[128,1]{0,1:T(1,128)S(1)}, bf16[128,2048]{1,0:T(8,128)(2,1)}, f32[1,128,16,128]{3,2,1,0:T(8,128)}, f32[1,1...) conditional(s32[]{:T(128)} %convert_element_type.277, () %tuple.40, ...), branch_computations={%region_0.1_spmd, %region_1.8_spmd} | conditional | flops 13036057600 | bytes 205435584 | solution.py:294
  1680.2 5.0 convolution_bitcast_fusion
  1695.6 5.9 multiply_reduce_fusion
  1703.7 13.4 fusion.84
  1717.1 15.5 multiply_convert_fusion
  1732.7 13.2 fusion
  1754.0 23.1 conditional.5
  1777.8 22.9 conditional.6
  1802.2 157.5 %collective-permute-done.4 = bf16[128,2048]{1,0:T(8,128)(2,1)} collective-permute-done((bf16[128,2048]{1,0:T(8,128)(2,1)S(1)}, bf16[128,2048]{1,0:T(8,128)(2,1)}, u32[]{:S(2)}, u32[]{:S(2)}) %collective-permute-start.4) | collective-permute-done | bytes 524320 | tf_op jit(solution)/shard_map/ppermute | solution.py:27
  1959.7 116.3 %conditional.7 = (bf16[128,2048]{0,1:T(8,128)(2,1)}, bf16[128,1024]{0,1:T(8,128)(2,1)}, bf16[128,1024]{0,1:T(8,128)(2,1)}, f32[2048]{0:T(1024)}, f32[128]{0:T(12...) conditional(s32[]{:T(128)} %convert_element_type.277, () %tuple.44, ...), branch_computations={%region_27.28_spmd, %region_28.38_spmd} | conditional | flops 13252196352 | bytes 241408736 | solution.py:308
  1959.7 16.1 multiply_convert_fusion.9
  1975.8 14.3 fusion.88
  1990.1 14.9 multiply_reduce_fusion.17
  2008.0 7.1 convolution_convert_fusion.5
  2043.5 6.6 fusion.89
  2098.3 12.3 all-to-all-done.2
  2116.0 16.5 all-to-all-done.1
  2139.2 9.8 all-to-all-done
  2161.4 35.7 %all-to-all-done.3 = bf16[128,4,1536]{0,2,1:T(8,128)(2,1)S(1)} async-done(((bf16[128,4,1536]{0,2,1:T(8,128)(2,1)}), bf16[128,4,1536]{0,2,1:T(8,128)(2,1)S(1)}, u32[]{:S(2)}, u32[]{:S(2)}) %all-to-all-start.3) | async-done | bytes 1572896 | tf_op jit(solution)/shard_map/all_to_all | solution.py:319
  2197.8 11.5 all-gather.24.cloned.1.call-done
  2209.3 4.4 fusion.75
  2213.7 43.3 %all-gather.30.cloned.1.call-done = bf16[512,2048]{0,1:T(8,128)(2,1)} async-done(((bf16[128,2048]{0,1:T(8,128)(2,1)}), bf16[512,2048]{0,1:T(8,128)(2,1)}) %all-gather.30.cloned.1.call-update) | async-done | bytes 2097168 | tf_op jit(solution)/shard_map/all_gather | solution.py:325
  2261.3 41.8 %all-gather.36.cloned.1.call-done = bf16[512,2048]{0,1:T(8,128)(2,1)} async-done(((bf16[128,2048]{0,1:T(8,128)(2,1)}), bf16[512,2048]{0,1:T(8,128)(2,1)}) %all-gather.36.cloned.1.call-update) | async-done | bytes 2097168 | tf_op jit(solution)/shard_map/all_gather | solution.py:328
  2303.1 7.0 fusion.74
  2310.1 108.0 %all-gather.34.cloned.1.call-done = bf16[512,6144]{0,1:T(8,128)(2,1)} async-done(((bf16[128,6144]{0,1:T(8,128)(2,1)}), bf16[512,6144]{0,1:T(8,128)(2,1)}) %all-gather.34.cloned.1.call-update) | async-done | bytes 6291472 | tf_op jit(solution)/shard_map/all_gather | solution.py:327
  2418.1 8.2 fusion.73
  2426.3 107.0 %all-gather.32.cloned.1.call-done = bf16[512,6144]{0,1:T(8,128)(2,1)} async-done(((bf16[128,6144]{0,1:T(8,128)(2,1)}), bf16[512,6144]{0,1:T(8,128)(2,1)}) %all-gather.32.cloned.1.call-update) | async-done | bytes 6291472 | tf_op jit(solution)/shard_map/all_gather | solution.py:326
  2533.3 8.2 fusion.72
  2546.8 16.6 all-reduce.6
  2563.7 10.5 all-reduce.7
  2579.0 404.6 %all-reduce.12.cloned.1.call-done = (bf16[1,512,2048]{2,1,0:T(8,128)(2,1)}, bf16[1,512,1024]{2,1,0:T(8,128)(2,1)}, bf16[1,512,1024]{2,1,0:T(8,128)(2,1)}, bf16[1...) async-done(((bf16[1,512,2048]{2,1,0:T(8,128)(2,1)}, bf16[1,512,1024]{2,1,0:T(8,128)(2,1)}, ...) | async-done | bytes 25165840 | tf_op jit(solution)/shard_map/psum | solution.py:351
  2983.7 9.4 broadcast_in_dim.187
  2993.0 6.4 broadcast_in_dim.189
  2999.5 6.3 broadcast_in_dim.191
  (357 shorter events, 192.3 us)
Async XLA Ops:
  7.2 903.0 %all-gather.40.cloned.1.call-start = ((), (), s32[]{:S(2)}) async-start(), calls=%async_computation.12 | async-start | bytes 5242880 | tf_op jit(solution)/shard_map/all_gather | solution.py:277
  7.9 902.3 %all-gather.42.cloned.1.call-start = ((), (), s32[]{:S(2)}) async-start(), calls=%async_computation.13 | async-start | bytes 5242880 | tf_op jit(solution)/shard_map/all_gather | solution.py:278
  8.7 901.5 %all-gather.38.cloned.1.call-start = ((), (), s32[]{:S(2)}) async-start(), calls=%async_computation.11 | async-start | bytes 10485760 | tf_op jit(solution)/shard_map/all_gather | solution.py:276
  9.4 900.8 %all-gather.44.cloned.1.call-start = ((), (), s32[]{:S(2)}) async-start(), calls=%async_computation.14 | async-start | bytes 10485760 | tf_op jit(solution)/shard_map/all_gather | solution.py:281
  10.0 1244.9 %all-gather.46.cloned.1.call-start = ((), (), s32[]{:S(2)}) async-start(), calls=%async_computation.15 | async-start | bytes 31457280 | tf_op jit(solution)/shard_map/all_gather | solution.py:283
  10.6 278.2 %copy-start.87 = (bf16[1,512]{1,0:T(2,128)(2,1)S(1)}, bf16[1,512]{1,0:T(2,128)(2,1)}, u32[]{:S(2)}) copy-start(bf16[1,512]{1,0:T(2,128)(2,1)} %param.23) | copy-start | bytes 3076
  10.6 796.1 %copy-start.88 = (bf16[1,512]{1,0:T(2,128)(2,1)S(1)}, bf16[1,512]{1,0:T(2,128)(2,1)}, u32[]{:S(2)}) copy-start(bf16[1,512]{1,0:T(2,128)(2,1)} %param.30) | copy-start | bytes 3076
  10.6 817.2 %copy-start.89 = (u32[32]{0:T(128)S(1)}, u32[32]{0:T(128)}, u32[]{:S(2)}) copy-start(u32[32]{0:T(128)} %constant.184) | copy-start | bytes 388
  10.6 818.5 %copy-start.100 = (bf16[1,32]{1,0:T(2,128)(2,1)S(1)}, bf16[1,32]{1,0:T(2,128)(2,1)}, u32[]{:S(2)}) copy-start(bf16[1,32]{1,0:T(2,128)(2,1)} %param.27) | copy-start | bytes 196
  10.6 818.7 %copy-start.101 = (bf16[1,32]{1,0:T(2,128)(2,1)S(1)}, bf16[1,32]{1,0:T(2,128)(2,1)}, u32[]{:S(2)}) copy-start(bf16[1,32]{1,0:T(2,128)(2,1)} %param.28) | copy-start | bytes 196
  10.6 1669.1 %all-gather.48.cloned.1.call-start = ((), (), s32[]{:S(2)}) async-start(), calls=%async_computation.16 | async-start | bytes 31457280 | tf_op jit(solution)/shard_map/all_gather | solution.py:284
  11.2 2144.1 %all-gather.28.cloned.1.call-start = ((), (), s32[]{:S(2)}) async-start(), calls=%async_computation.6 | async-start | bytes 1310720 | tf_op jit(solution)/shard_map/all_gather | solution.py:324
  11.2 255.8 %collective-permute-start = (bf16[1536,2048]{1,0:T(8,128)(2,1)}, bf16[1536,2048]{1,0:T(8,128)(2,1)}, u32[]{:S(2)}, u32[]{:S(2)}) collective-permute-start(bf16[1536,2048]{1,0:T(8,128)(2,1)} %bitcast.445), channel_id=1, source_target_pairs={{0,4},{4,8},{8,12},{12,0},{1,5},{5,9},{9,13},{13,1},{2,6},{6,10},{... | collective-permute-start | bytes 18874376 | tf_op jit(solution)/shard_map/ppermute | solution.py:17
  267.1 572.3 %collective-permute-start.1 = (bf16[1536,2048]{1,0:T(8,128)(2,1)}, bf16[1536,2048]{1,0:T(8,128)(2,1)}, u32[]{:S(2)}, u32[]{:S(2)}) collective-permute-start(bf16[1536,2048]{1,0:T(8,128)(2,1)} %collective-permute-done), channel_id=1, source_target_pairs={{0,4},{4,8},{8,12},{12,0},{1,5},{5,9},{9,13},{13,1},{2,6},{6,10},{... | collective-permute-start | bytes 18874376 | tf_op jit(solution)/shard_map/ppermute | solution.py:17
  285.8 572.4 %collective-permute-start.2 = (bf16[1536,2048]{1,0:T(8,128)(2,1)}, bf16[1536,2048]{1,0:T(8,128)(2,1)}, u32[]{:S(2)}, u32[]{:S(2)}) collective-permute-start(bf16[1536,2048]{1,0:T(8,128)(2,1)} %bitcast.446), channel_id=1, source_target_pairs={{0,12},{4,0},{8,4},{12,8},{1,13},{5,1},{9,5},{13,9},{2,14},{6,2},{... | collective-permute-start | bytes 18874376 | tf_op jit(solution)/shard_map/ppermute | solution.py:19
  839.4 914.5 %copy-start.102 = (bf16[128]{0:T(256)(128)(2,1)}, bf16[128]{0:T(256)(128)(2,1)S(1)}, u32[]{:S(2)}) copy-start(bf16[128]{0:T(256)(128)(2,1)S(1)} %get-tuple-element.1148) | copy-start | bytes 772
  839.4 914.5 %copy-start.103 = (bf16[128]{0:T(256)(128)(2,1)}, bf16[128]{0:T(256)(128)(2,1)S(1)}, u32[]{:S(2)}) copy-start(bf16[128]{0:T(256)(128)(2,1)S(1)} %get-tuple-element.1149) | copy-start | bytes 772
  839.4 15.7 slice-start
  887.7 792.0 %copy-start.65 = (bf16[128,2048]{1,0:T(8,128)(2,1)S(1)}, bf16[128,2048]{1,0:T(8,128)(2,1)}, u32[]{:S(2)}) copy-start(bf16[128,2048]{1,0:T(8,128)(2,1)} %param.21) | copy-start | bytes 1572868
  1680.0 15.6 copy-start.8
  1732.7 15.3 copy-start.38
  1732.7 15.3 copy-start.40
  1732.7 17.5 copy-start.53
  1732.7 17.5 copy-start.55
  1732.7 17.7 copy-start.58
  1732.7 17.7 copy-start.9
  1750.9 3.0 collective-permute-start.3
  1777.8 181.9 %copy-start.13 = (f32[1,128,16,128]{3,2,1,0:T(8,128)S(1)}, f32[1,128,16,128]{3,2,1,0:T(8,128)}, u32[]{:S(2)}) copy-start(f32[1,128,16,128]{3,2,1,0:T(8,128)} %get-tuple-element.366) | copy-start | bytes 3145732
  1777.8 181.9 %copy-start.70 = (f32[1,128,16,1]{2,1,3,0:T(8,128)S(1)}, f32[1,128,16,1]{2,1,3,0:T(8,128)}, u32[]{:S(2)}) copy-start(f32[1,128,16,1]{2,1,3,0:T(8,128)} %copy-done.69) | copy-start | bytes 24580
  1800.8 158.9 %copy-start.23 = (f32[128,2048]{1,0:T(8,128)}, f32[128,2048]{1,0:T(8,128)S(1)}, u32[]{:S(2)}) copy-start(f32[128,2048]{1,0:T(8,128)S(1)} %get-tuple-element.355) | copy-start | bytes 3145732
  1800.9 158.8 %collective-permute-start.4 = (bf16[128,2048]{1,0:T(8,128)(2,1)S(1)}, bf16[128,2048]{1,0:T(8,128)(2,1)}, u32[]{:S(2)}, u32[]{:S(2)}) collective-permute-start(bf16[128,2048]{1,0:T(8,128)(2,1)S(1)} %convert_element_type.279), channel_id=1, source_target_pairs={{16,0},{17,1},{18,2},{19,3},{20,4},{21,5},{22,6},{23,7},{24,8},{25... | collective-permute-start | bytes 1572872 | tf_op jit(solution)/shard_map/ppermute | solution.py:27
  1975.8 14.3 copy-start.82
  2008.0 14.0 copy-start.73
  2077.7 80.7 %all-gather.26.cloned.1.call-start = ((), (), s32[]{:S(2)}) async-start(), calls=%async_computation.5 | async-start | bytes 1310720 | tf_op jit(solution)/shard_map/all_gather | solution.py:323
  2079.5 129.9 %all-gather.24.cloned.1.call-start = ((), (), s32[]{:S(2)}) async-start(), calls=%async_computation.4 | async-start | bytes 2621440 | tf_op jit(solution)/shard_map/all_gather | solution.py:322
  2081.4 175.6 %all-gather.30.cloned.1.call-start = ((), (), s32[]{:S(2)}) async-start(), calls=%async_computation.7 | async-start | bytes 2621440 | tf_op jit(solution)/shard_map/all_gather | solution.py:325
  2083.4 219.7 %all-gather.36.cloned.1.call-start = ((), (), s32[]{:S(2)}) async-start(), calls=%async_computation.10 | async-start | bytes 2621440 | tf_op jit(solution)/shard_map/all_gather | solution.py:328
  2085.4 332.7 %all-gather.34.cloned.1.call-start = ((), (), s32[]{:S(2)}) async-start(), calls=%async_computation.9 | async-start | bytes 7864320 | tf_op jit(solution)/shard_map/all_gather | solution.py:327
  2088.2 445.1 %all-gather.32.cloned.1.call-start = ((), (), s32[]{:S(2)}) async-start(), calls=%async_computation.8 | async-start | bytes 7864320 | tf_op jit(solution)/shard_map/all_gather | solution.py:326
  2092.9 17.7 all-to-all-start.2
  2110.6 21.9 all-to-all-start.1
  2132.5 16.6 all-to-all-start
  2149.1 48.0 %all-to-all-start.3 = ((bf16[128,4,1536]{0,2,1:T(8,128)(2,1)}), bf16[128,4,1536]{0,2,1:T(8,128)(2,1)S(1)}, u32[]{:S(2)}, u32[]{:S(2)}) async-start(bf16[128,4,1536]{0,2,1:T(8,128)(2,1)} %bitcast.171), calls=%async_computation.3 | async-start | bytes 3145728 | tf_op jit(solution)/shard_map/all_to_all | solution.py:319
  2153.0 830.6 %all-reduce.12.cloned.1.call-start = ((), (), s32[]{:S(2)}) async-start(), calls=%async_computation.17 | async-start | bytes 50331648 | tf_op jit(solution)/shard_map/psum | solution.py:351
  2155.3 41.9 %copy-start.68 = (bf16[4,128,512]{2,1,0:T(8,128)(2,1)}, bf16[4,128,512]{2,1,0:T(8,128)(2,1)S(1)}, u32[]{:S(2)}) copy-start(bf16[4,128,512]{2,1,0:T(8,128)(2,1)S(1)} %copy.316) | copy-start | bytes 1572868
  2197.8 59.2 %copy-start.67 = (bf16[4,128,512]{2,1,0:T(8,128)(2,1)S(1)}, bf16[4,128,512]{2,1,0:T(8,128)(2,1)}, u32[]{:S(2)}) copy-start(bf16[4,128,512]{2,1,0:T(8,128)(2,1)} %copy.319) | copy-start | bytes 1572868
  2303.1 115.0 %copy-start.66 = (bf16[4,128,512]{2,1,0:T(8,128)(2,1)S(1)}, bf16[4,128,512]{2,1,0:T(8,128)(2,1)}, u32[]{:S(2)}) copy-start(bf16[4,128,512]{2,1,0:T(8,128)(2,1)} %copy.324) | copy-start | bytes 1572868
  2983.7 15.8 slice-start.2
  (50 other events, 216.9 us)
Sparse Core Ops, SparseCore 0:
  9.6 150.7 all-gather.39
  161.9 125.4 all-gather.41
  289.0 337.2 all-gather.37
  627.7 200.9 all-gather.43
  830.2 424.6 all-gather.45
  1256.3 423.3 all-gather.47
  2077.8 31.9 all-gather.27
  2111.9 34.5 all-gather.25
  2148.7 60.6 all-gather.23
  2210.8 46.2 all-gather.29
  2258.6 44.4 all-gather.35
  2305.1 112.9 all-gather.33
  2420.2 112.9 all-gather.31
  2541.6 441.9 all-reduce.11
